TPU v7x, 32 devices: a whole 2x2x4 slice. The times are simulated.
32 devices in a mesh: data: 32 (over z, y, x, core).
Axes of the slice: x: 2, y: 2, z: 4, core: 2. Of those that a mesh axis runs over, the one named last changes fastest.
Arguments:
- act_in: bfloat16 [16384, 2560], P('data')
- grad_out: bfloat16 [16384, 2560], P('data')
- w_up: bfloat16 [2, 2560, 6912], replicated
- w_down: bfloat16 [2, 6912, 2560], replicated
- q_up: bfloat16 [2, 6912, 512], replicated
- q_down: bfloat16 [2, 2560, 512], replicated
Outputs:
- output 1: bfloat16 [2, 2560, 6912], replicated
- output 2: bfloat16 [2, 6912, 2560], replicated
- output 3: float32 [2, 6912, 512], replicated
- output 4: float32 [2, 2560, 512], replicated
All inputs are finite; a program needn't handle non-finite values.
Results may differ from a plain program's by a relative error of at most 0.00803997.
Values are sent between devices in bfloat16 or wider.
A program may use at most 1.5 GiB of HBM per device.

v0:
```python
import math
import jax
import jax.numpy as jnp
from jax import lax
from jax.sharding import PartitionSpec as P, NamedSharding


def gelu_tanh(values):
    return jax.nn.gelu(values, approximate=True)


def gelu_grad(pre_gelu, cot_gelu):
    pull_back = jax.vjp(gelu_tanh, pre_gelu)[1]
    return pull_back(cot_gelu)[0]


def mat_nn(left_op, right_op):
    return jnp.dot(left_op, right_op, preferred_element_type=jnp.float32)


def mat_nt(left_op, right_op):
    return lax.dot_general(left_op, right_op, (((1,), (1,)), ((), ())), preferred_element_type=jnp.float32)


def mat_tn(left_op, right_op):
    return lax.dot_general(left_op, right_op, (((0,), (0,)), ((), ())), preferred_element_type=jnp.float32)


def block_pairs(tok_rows, grad_rows, w_up, w_down):
    layers = w_up.shape[0]
    hiddens = []
    pre_gelus = []
    gelu_outs = []
    hidden = tok_rows
    for layer in range(layers):
        hiddens.append(hidden)
        pre_gelu = mat_nn(hidden, w_up[layer]).astype(jnp.bfloat16)
        gelu_out = gelu_tanh(pre_gelu.astype(jnp.float32)).astype(jnp.bfloat16)
        pre_gelus.append(pre_gelu)
        gelu_outs.append(gelu_out)
        if layer + 1 < layers:
            hidden = (hidden.astype(jnp.float32) + mat_nn(gelu_out, w_down[layer])).astype(jnp.bfloat16)
    up_pairs = [None] * layers
    down_pairs = [None] * layers
    cot_hidden = grad_rows
    for layer in reversed(range(layers)):
        down_pairs[layer] = (gelu_outs[layer], cot_hidden)
        cot_gelu = mat_nt(cot_hidden, w_down[layer])
        cot_pre = gelu_grad(pre_gelus[layer].astype(jnp.float32), cot_gelu).astype(jnp.bfloat16)
        up_pairs[layer] = (hiddens[layer], cot_pre)
        if layer > 0:
            cot_hidden = (cot_hidden.astype(jnp.float32) + mat_nt(cot_pre, w_up[layer])).astype(jnp.bfloat16)
    return up_pairs, down_pairs


def col_normalise(p_sum):
    return (p_sum / jnp.sqrt(jnp.sum(p_sum * p_sum, axis=-2, keepdims=True))).astype(jnp.bfloat16)


def apply_update(weight, p_hat, q_sum, step_size):
    return (weight.astype(jnp.float32) - step_size * mat_nt(p_hat, q_sum.astype(jnp.bfloat16))).astype(jnp.bfloat16)


def power_step(row_pair, q_fac, weight, step_size, data_axis):
    left_in, right_in = row_pair
    sketch = mat_nn(right_in, q_fac).astype(jnp.bfloat16)
    p_sum = lax.psum(mat_tn(left_in, sketch), data_axis)
    p_hat = col_normalise(p_sum)
    back_in = mat_nn(left_in, p_hat).astype(jnp.bfloat16)
    q_sum = lax.psum(mat_tn(right_in, back_in), data_axis)
    return apply_update(weight, p_hat, q_sum, step_size), q_sum


def solution(mesh):
    data_axis = mesh.axis_names[0]

    def local_step(tok_rows, grad_rows, w_up, w_down, q_up, q_down):
        step_size = 0.4 / math.sqrt(q_up.shape[-1])
        up_pairs, down_pairs = block_pairs(tok_rows, grad_rows, w_up, w_down)
        up_new, down_new, up_fac, down_fac = [], [], [], []
        for layer in range(w_up.shape[0]):
            new_weight, q_sum = power_step(up_pairs[layer], q_up[layer], w_up[layer], step_size, data_axis)
            up_new.append(new_weight)
            up_fac.append(q_sum)
            new_weight, q_sum = power_step(down_pairs[layer], q_down[layer], w_down[layer], step_size, data_axis)
            down_new.append(new_weight)
            down_fac.append(q_sum)
        return jnp.stack(up_new), jnp.stack(down_new), jnp.stack(up_fac), jnp.stack(down_fac)

    row_spec = P(data_axis, None)
    return jax.shard_map(local_step, mesh=mesh, in_specs=(row_spec, row_spec, P(), P(), P(), P()), out_specs=(P(), P(), P(), P()), check_vma=False)
```

profile of v0, /device:TPU:0, one launch (start us, length us, event | category | flops | bytes accessed | tf_op | source)
XLA Modules:
  0.0 1739.3 jit_solution(2078846989680446534)
XLA Ops:
  7.2 0.0 copy-start.3
  7.2 0.0 all-reduce.7.cloned.1.call-start
  7.2 28.5 %fusion.42 = bf16[512,6912]{1,0:T(8,128)(2,1)} fusion(bf16[512,2560]{1,0:T(8,128)(2,1)} %param.6, bf16[2,2560,6912]{2,1,0:T(8,128)(2,1)} %param.8), kind=kOutput, calls=%fused_computation.63 | convolution fusion | flops 18122932224 | bytes 45088768 | tf_op jit(solution)/shard_map/dot_general | solution.py:18
  35.7 0.0 copy-done.3
  35.7 34.4 %add_convert_fusion.1 = bf16[512,2560]{1,0:T(8,128)(2,1)} fusion(bf16[512,2560]{1,0:T(8,128)(2,1)S(1)} %copy-done.3, bf16[2,6912,2560]{2,1,0:T(8,128)(2,1)} %param.9, bf16[512,6912]{1,0:T(8,128)(2,1)} %fusion.42), kind=kOutput, calls=%fused_computation.79 | convolution fusion | flops 18158714880 | bytes 47710208 | tf_op jit(solution)/shard_map/dot_general | solution.py:18
  70.1 0.0 copy-start.1
  70.1 25.6 %fusion.45 = bf16[512,6912]{1,0:T(8,128)(2,1)} fusion(bf16[512,2560]{1,0:T(8,128)(2,1)} %add_convert_fusion.1, bf16[2,2560,6912]{2,1,0:T(8,128)(2,1)} %param.8), kind=kOutput, calls=%fused_computation.64 | convolution fusion | flops 18122932224 | bytes 45088768 | tf_op jit(solution)/shard_map/dot_general | solution.py:18
  95.7 0.0 copy-done.1
  95.7 32.0 %fusion.26 = bf16[512,6912]{1,0:T(8,128)(2,1)} fusion(bf16[512,6912]{1,0:T(8,128)(2,1)} %fusion.45, bf16[512,2560]{1,0:T(8,128)(2,1)S(1)} %copy-done.1, bf16[2,6912,2560]{2,1,0:T(8,128)(2,1)} %param.9), kind=kOutput, calls=%fused_computation.43 | convolution fusion | flops 18193711104 | bytes 52166656 | tf_op jit(solution)/shard_map/dot_general | solution.py:22
  127.7 25.2 %add_convert_fusion = bf16[512,2560]{1,0:T(8,128)(2,1)} fusion(bf16[512,2560]{1,0:T(8,128)(2,1)S(1)} %copy-done.1, bf16[512,6912]{1,0:T(8,128)(2,1)} %fusion.26, bf16[2,2560,6912]{2,1,0:T(8,128)(2,1)} %param.8), kind=kOutput, calls=%fused_computation.78 | convolution fusion | flops 18123325440 | bytes 47710208 | tf_op jit(solution)/shard_map/dot_general | solution.py:22
  152.9 32.9 %fusion.29 = bf16[512,6912]{1,0:T(8,128)(2,1)} fusion(bf16[512,6912]{1,0:T(8,128)(2,1)} %fusion.42, bf16[512,2560]{1,0:T(8,128)(2,1)} %add_convert_fusion, bf16[2,6912,2560]{2,1,0:T(8,128)(2,1)} %param.9), kind=kOutput, calls=%fused_computation.46 | convolution fusion | flops 18193711104 | bytes 52166656 | tf_op jit(solution)/shard_map/dot_general | solution.py:22
  185.8 16.1 fusion.82
  201.9 15.7 fusion.88
  217.6 0.0 copy-start.4
  217.6 13.5 fusion.100
  231.2 0.0 copy-done.4
  231.2 12.6 convolution_bitcast_fusion.1
  243.8 0.0 all-reduce.7.cloned.1.call-update
  243.8 0.0 all-reduce.5.cloned.1.call-start
  243.9 564.0 %all-reduce.7.cloned.1.call-done = (f32[2560,512]{1,0:T(8,128)}, f32[2560,512]{0,1:T(8,128)}, f32[6912,512]{1,0:T(8,128)}, f32[6912,512]{1,0:T(8,128)}) async-done(((f32[2560,512]{1,0:T(8,128)}, f32[2560,512]{0,1:T(8,128)}, f32[6912,512]{1,0:T(8,128)}, f32[6912,512]{1,0:T(8,128)}), (f32[2560,512]{1,0:T(8,128)}, f32[2560,512]{0,1:T(8,128)}, f32[6912,512]{1,0:T(8,128)}, ...) | async-done | bytes 38797328 | tf_op jit(solution)/shard_map/psum | solution.py:67
  807.8 0.0 copy-start
  807.9 6.2 multiply_reduce_fusion
  814.0 6.7 multiply_reduce_fusion.1
  820.7 0.2 copy-done
  820.9 10.9 divide_convert_fusion
  831.8 0.0 copy-start.2
  831.8 14.7 fusion.101
  846.5 0.0 copy-done.2
  846.5 14.1 convolution_bitcast_fusion
  860.5 2.9 multiply_reduce_fusion.2
  863.4 2.9 multiply_reduce_fusion.3
  866.4 0.0 copy-start.5
  866.4 16.0 fusion.90
  882.4 0.0 copy-done.5
  882.4 12.6 fusion.91
  895.0 0.0 all-reduce.5.cloned.1.call-update
  895.1 561.5 %all-reduce.5.cloned.1.call-done = (f32[6912,512]{1,0:T(8,128)}, f32[6912,512]{1,0:T(8,128)}, f32[2560,512]{1,0:T(8,128)}, f32[2560,512]{1,0:T(8,128)}) async-done(((f32[6912,512]{1,0:T(8,128)}, f32[6912,512]{1,0:T(8,128)}, f32[2560,512]{1,0:T(8,128)}, f32[2560,512]{1,0:T(8,128)}), (f32[6912,512]{1,0:T(8,128)}, f32[6912,512]{1,0:T(8,128)}, f32[2560,512]{1,0:T(8,128)}, ...) | async-done | bytes 38797328 | tf_op jit(solution)/shard_map/psum | solution.py:70
  1456.5 36.6 %fusion.15 = bf16[1,6912,2560]{2,1,0:T(8,128)(2,1)} fusion(bf16[6912,512]{1,0:T(8,128)(2,1)} %get-tuple-element.12, bf16[2,6912,2560]{2,1,0:T(8,128)(2,1)} %param.9, f32[2560,512]{1,0:T(8,128)} %get-tuple-element.6), kind=kOutput, calls=%fused_computation.21 | convolution fusion | flops 18191482880 | bytes 83099648 | tf_op jit(solution)/shard_map/dot_general | solution.py:22
  1493.2 36.3 %fusion.14 = bf16[1,6912,2560]{2,1,0:T(8,128)(2,1)} fusion(bf16[6912,512]{1,0:T(8,128)(2,1)} %get-tuple-element.13, bf16[2,6912,2560]{2,1,0:T(8,128)(2,1)} %param.9, f32[2560,512]{1,0:T(8,128)} %get-tuple-element.7), kind=kOutput, calls=%fused_computation.20 | convolution fusion | flops 18191482880 | bytes 83099648 | tf_op jit(solution)/shard_map/dot_general | solution.py:22
  1529.4 39.1 %fusion.13 = bf16[1,2560,6912]{2,1,0:T(8,128)(2,1)} fusion(bf16[2,2560,6912]{2,1,0:T(8,128)(2,1)} %param.8, f32[6912,512]{1,0:T(8,128)} %get-tuple-element.4, f32[2560,512]{1,0:T(8,128)} %get-tuple-element.8, f32[512]{0:T(512)S(1)} %sqrt.33), kind=kOutput, calls=%fused_computation.19 | convolution fusion | flops 18196332544 | bytes 90179584 | tf_op jit(solution)/shard_map/dot_general | solution.py:22
  1568.5 38.7 %fusion.12 = bf16[1,2560,6912]{2,1,0:T(8,128)(2,1)} fusion(bf16[2,2560,6912]{2,1,0:T(8,128)(2,1)} %param.8, f32[6912,512]{1,0:T(8,128)} %get-tuple-element.5, f32[2560,512]{0,1:T(8,128)} %get-tuple-element.9, f32[512]{0:T(512)S(1)} %sqrt.32), kind=kOutput, calls=%fused_computation.18 | convolution fusion | flops 18196332544 | bytes 90179584 | tf_op jit(solution)/shard_map/dot_general | solution.py:22
  1607.3 9.4 pad_maximum_fusion.3
  1616.7 22.0 %pad_maximum_fusion.2 = f32[2,6912,512]{2,1,0:T(8,128)} fusion(f32[1,6912,512]{2,1,0:T(8,128)} %bitcast.131, f32[1,6912,512]{2,1,0:T(8,128)} %bitcast.132), kind=kLoop, calls=%fused_computation.24 | loop fusion | flops 7077888 | bytes 56623104 | tf_op jit(solution)/shard_map/stack | solution.py:88
  1638.6 46.9 %pad_maximum_fusion.1 = bf16[2,6912,2560]{2,1,0:T(8,128)(2,1)} fusion(bf16[1,6912,2560]{2,1,0:T(8,128)(2,1)} %fusion.15, bf16[1,6912,2560]{2,1,0:T(8,128)(2,1)} %fusion.14), kind=kLoop, calls=%fused_computation.1 | loop fusion | flops 35389440 | bytes 141557760 | tf_op jit(solution)/shard_map/stack | solution.py:88
  1685.5 46.7 %pad_maximum_fusion = bf16[2,2560,6912]{2,1,0:T(8,128)(2,1)} fusion(bf16[1,2560,6912]{2,1,0:T(8,128)(2,1)} %fusion.13, bf16[1,2560,6912]{2,1,0:T(8,128)(2,1)} %fusion.12), kind=kLoop, calls=%fused_computation | loop fusion | flops 35389440 | bytes 141557760 | tf_op jit(solution)/shard_map/stack | solution.py:88
  (4 shorter events, 0.0 us)
Async XLA Ops:
  7.2 28.6 %copy-start.3 = (bf16[512,2560]{1,0:T(8,128)(2,1)S(1)}, bf16[512,2560]{1,0:T(8,128)(2,1)}, u32[]{:S(2)}) copy-start(bf16[512,2560]{1,0:T(8,128)(2,1)} %param.6) | copy-start | bytes 7864324
  7.2 800.7 %all-reduce.7.cloned.1.call-start = ((), (), s32[]{:S(2)}) async-start(), calls=%async_computation.1 | async-start | bytes 77594624 | tf_op jit(solution)/shard_map/psum | solution.py:67
  70.1 25.6 %copy-start.1 = (bf16[512,2560]{1,0:T(8,128)(2,1)S(1)}, bf16[512,2560]{1,0:T(8,128)(2,1)}, u32[]{:S(2)}) copy-start(bf16[512,2560]{1,0:T(8,128)(2,1)} %param.7) | copy-start | bytes 7864324
  217.6 13.6 copy-start.4
  243.8 1212.7 %all-reduce.5.cloned.1.call-start = ((), (), s32[]{:S(2)}) async-start(), calls=%async_computation | async-start | bytes 77594624 | tf_op jit(solution)/shard_map/psum | solution.py:70
  807.8 13.1 copy-start
  831.8 14.7 copy-start.2
  866.4 16.0 copy-start.5
Sparse Core Ops, SparseCore 0:
  243.9 563.8 all-reduce.6
  895.2 561.3 all-reduce.4
where the time goes:
time: 1740 us
  waiting for transfers between devices  1130 us (65%)
  matrix products  445 us (26%)
  other arithmetic  154 us (9%)
    psum x1, waiting for transfers between devices, power_step(): p_sum = lax.psum(mat_tn(left_in, sketch), data_axis)  564 us
    psum x1, waiting for transfers between devices, power_step(): q_sum = lax.psum(mat_tn(right_in, back_in), data_axis)  561 us
    dot_general x7, matrix products, mat_nt(): lax.dot_general(left_op, right_op, (((1,), (1,)), ((), ())), preferred_el...  241 us
    dot_general x8, matrix products, mat_tn(): lax.dot_general(left_op, right_op, (((0,), (0,)), ((), ())), preferred_el...  115 us
    dot_general x3, matrix products, mat_nn(): return jnp.dot(left_op, right_op, preferred_element_type=jnp.float32)  88.5 us
    another operation x1, other arithmetic, local_step(): jnp.stack(down_new)  46.9 us
    another operation x1, other arithmetic, local_step(): jnp.stack(up_new)  46.7 us
  transfers between devices with their start and end apart: 2, of which 2 were waited for; matrix products, arithmetic and copies ran while one was open for 0% of the time, Pallas kernels for 0%

commit v1 on v0

v1 whole, which is shorter than its diff:
```python
import math
import functools
import jax
import jax.numpy as jnp
from jax import lax
from jax.experimental import pallas as pl
from jax.experimental.pallas import tpu as pltpu

MESH = pl.DeviceIdType.MESH
CYCLES = (
    (0, 1, 3, 2, 6, 7, 5, 9, 11, 10, 14, 15, 13, 12, 8, 4),
    (0, 1, 5, 4, 6, 10, 8, 9, 13, 12, 14, 15, 11, 7, 3, 2),
    (0, 2, 6, 7, 3, 1, 5, 9, 13, 15, 11, 10, 14, 12, 8, 4),
)
RINGS = tuple((j, d) for j in range(3) for d in range(2))
CHIPS = 16


def pick(table, index):
    value = jnp.int32(table[0])
    for k in range(1, len(table)):
        value = jnp.where(index == k, jnp.int32(table[k]), value)
    return value


def inverse(table):
    return tuple(table.index(k) for k in range(len(table)))


class Place:
    def __init__(self):
        me = lax.axis_index("data")
        self.core = lax.rem(me, 2)
        self.chip = lax.div(me, 2)
        self.partner = me + 1 - 2 * self.core
        self.pos = [pick(inverse(c), self.chip) for c in CYCLES]
        self.ahead = [2 * pick(c, lax.rem(p + 1, CHIPS)) + self.core for c, p in zip(CYCLES, self.pos)]
        self.behind = [2 * pick(c, lax.rem(p + CHIPS - 1, CHIPS)) + self.core for c, p in zip(CYCLES, self.pos)]

    def target(self, j, d):
        return self.ahead[j] if d == 0 else self.behind[j]

    def owner(self, j, d, back):
        p = self.pos[j]
        index = lax.rem(p + 2 * CHIPS - back, CHIPS) if d == 0 else lax.rem(p + back, CHIPS)
        return pick(CYCLES[j], index)

    def barrier(self):
        sem = pltpu.get_barrier_semaphore()
        for dev in (*self.ahead, *self.behind, self.partner):
            pl.semaphore_signal(sem, inc=1, device_id=(dev,), device_id_type=MESH)
        pl.semaphore_wait(sem, 7)


def remote(src, dst, send, recv, dev):
    return pltpu.make_async_remote_copy(src_ref=src, dst_ref=dst, send_sem=send, recv_sem=recv, device_id=(dev,), device_id_type=MESH)


def drain(ref, sem):
    pltpu.make_async_copy(ref, ref, sem).wait()


AHEAD = 3


def left_kernel(m1, m2, p1_ref, p2_ref, o1_ref, o2_ref, mine, part, slots, phat, stage_sem, pair_send, pair_recv, ring_send, ring_recv, gat_send, gat_recv, fwd_send, fwd_recv, out_sem):
    width = m1 + m2
    tiles = width // 128
    third = (tiles + 2) // 3 * 128
    cuts = (0, third, 2 * third, width)
    spans = tuple((cuts[j], cuts[j + 1] - cuts[j]) for j in range(3))
    here = Place()
    here.barrier()

    def pieces(j):
        start, size = spans[j]
        out = []
        if start < m1:
            out.append((p1_ref, start, start, min(size, m1 - start)))
        if start + size > m1:
            first = max(start, m1)
            out.append((p2_ref, first - m1, first, start + size - first))
        return out

    def stage(t):
        for j, d in RINGS:
            row = 16 * here.owner(j, d, t + 1) + 8 * d
            for ref, col, place, size in pieces(j):
                to = pl.ds(place, size)
                frm = pl.ds(col, size)
                pltpu.make_async_copy(ref.at[pl.ds(256 * here.core + row, 8), frm], mine.at[pl.ds(row, 8), to], stage_sem.at[t]).start()
                remote(ref.at[pl.ds(256 * (1 - here.core) + row, 8), frm], part.at[pl.ds(row, 8), to], pair_send.at[t], pair_recv.at[t], here.partner).start()

    def step(t, first, last):
        drain(mine.at[pl.ds(0, 16)], stage_sem.at[t])
        drain(part.at[pl.ds(0, 16)], pair_recv.at[t])
        for r, (j, d) in enumerate(RINGS):
            start, size = spans[j]
            row = 16 * here.owner(j, d, t + 1) + 8 * d
            block = mine.at[pl.ds(row, 8), pl.ds(start, size)]
            value = block[...] + part[pl.ds(row, 8), pl.ds(start, size)]
            if not first:
                slot = slots.at[t - 1, r, :, pl.ds(0, size)]
                drain(slot, ring_recv.at[t - 1, r])
                value = value + slot[...]
            block[...] = value
            if not last:
                remote(block, slots.at[t, r, :, pl.ds(0, size)], ring_send.at[t], ring_recv.at[t, r], here.target(j, d)).start()

    for t in range(AHEAD):
        stage(t)
    stage(AHEAD)
    step(0, True, False)

    def middle(t, carry):
        stage(t + AHEAD)
        step(t, False, False)
        return carry

    lax.fori_loop(1, CHIPS - AHEAD, middle, 0)
    lax.fori_loop(CHIPS - AHEAD, CHIPS - 1, lambda t, c: (step(t, False, False), c)[1], 0)
    step(CHIPS - 1, False, True)

    base = pl.multiple_of(16 * here.chip, 16)
    rows = pl.multiple_of(256 * here.core + base, 16)
    for lo, hi in ((0, m1), (m1, width)):
        total = jnp.zeros((16, 128), jnp.float32)
        for c in range(lo, hi, 128):
            v = mine[pl.ds(base, 16), pl.ds(c, 128)]
            total = total + v * v
        norm = jnp.sqrt(jnp.sum(total, axis=1, keepdims=True))
        for c in range(lo, hi, 256):
            phat[pl.ds(rows, 16), pl.ds(c, 256)] = (mine[pl.ds(base, 16), pl.ds(c, 256)] / norm).astype(jnp.bfloat16)

    group = (tiles + 5) // 6
    counts = [group if g < tiles - 6 * (group - 1) else group - 1 for g in range(6)]
    starts = [128 * sum(counts[:g]) for g in range(6)]

    def forward(row, cols, s, j, d, r, onward):
        block = phat.at[pl.ds(row, 16), cols]
        if onward:
            remote(block, block, gat_send.at[s], gat_recv.at[s, r], here.target(j, d)).start()
        remote(block, block, fwd_send.at[s], fwd_recv.at[s], here.partner).start()

    def gather_step(s, first, last):
        for r, (j, d) in enumerate(RINGS):
            row = pl.multiple_of(256 * here.core + 16 * here.owner(j, d, s), 16)
            cols = pl.ds(starts[r], 128 * counts[r])
            if not first:
                drain(phat.at[pl.ds(row, 16), cols], gat_recv.at[s - 1, r])
            forward(row, cols, s, j, d, r, not last)

    gather_step(0, True, False)
    lax.fori_loop(1, CHIPS - 1, lambda s, c: (gather_step(s, False, False), c)[1], 0)
    gather_step(CHIPS - 1, False, True)

    def flush_in(s, carry):
        drain(phat.at[pl.ds(0, 16)], fwd_recv.at[s])
        return carry

    lax.fori_loop(0, CHIPS, flush_in, 0)
    out1 = pltpu.make_async_copy(phat.at[:, pl.ds(0, m1)], o1_ref, out_sem.at[0])
    out2 = pltpu.make_async_copy(phat.at[:, pl.ds(m1, m2)], o2_ref, out_sem.at[1])
    out1.start()
    out2.start()

    def settle(s, carry):
        drain(mine.at[pl.ds(0, 16)], pair_send.at[s])
        drain(phat.at[pl.ds(0, 16)], fwd_send.at[s])
        return carry

    lax.fori_loop(0, CHIPS, settle, 0)

    def settle_rings(s, carry):
        drain(mine.at[pl.ds(0, 16)], ring_send.at[s])
        drain(phat.at[pl.ds(0, 16)], gat_send.at[s])
        return carry

    lax.fori_loop(0, CHIPS - 1, settle_rings, 0)
    out1.wait()
    out2.wait()


def left_exchange(p1, p2):
    rank, m1 = p1.shape
    m2 = p2.shape[1]
    width = m1 + m2
    third = (width // 128 + 2) // 3 * 128
    dma = pltpu.SemaphoreType.DMA
    return pl.pallas_call(
        functools.partial(left_kernel, m1, m2),
        out_shape=(jax.ShapeDtypeStruct((rank, m1), jnp.bfloat16), jax.ShapeDtypeStruct((rank, m2), jnp.bfloat16)),
        in_specs=[pl.BlockSpec(memory_space=pl.ANY)] * 2,
        out_specs=(pl.BlockSpec(memory_space=pl.ANY),) * 2,
        scratch_shapes=[
            pltpu.VMEM((256, width), jnp.float32),
            pltpu.VMEM((256, width), jnp.float32),
            pltpu.VMEM((15, 6, 8, third), jnp.float32),
            pltpu.VMEM((512, width), jnp.bfloat16),
            dma((16,)), dma((16,)), dma((16,)), dma((15,)), dma((15, 6)), dma((15,)), dma((15, 6)), dma((16,)), dma((16,)), dma((2,)),
        ],
        compiler_params=pltpu.CompilerParams(collective_id=0, has_side_effects=True, vmem_limit_bytes=60 * 2**20),
        name="left_exchange",
    )(p1, p2)


def right_kernel(n1, n2, q1_ref, q2_ref, o1_ref, o2_ref, mine, part, slots, stage_sem, pair_send, pair_recv, ring_send, ring_recv, gat_send, gat_recv, fwd_send, fwd_recv, out_sem):
    u1, u2 = n1 // 32, n2 // 32
    unit = u1 + u2
    w1 = u1 // 3
    second = (u2 - 16) // 16 * 8
    w2 = (u2 - 2 * second, second, second)
    from2 = (0, w2[0], w2[0] + second)
    sizes = tuple(w1 + w2[j] for j in range(3))
    offs = (0, sizes[0], sizes[0] + sizes[1])
    here = Place()
    here.barrier()

    def pieces(core, chip, j, d):
        base = unit * chip + offs[j]
        cols = pl.ds(256 * d, 256)
        row1 = pl.multiple_of((n1 // 2) * core + u1 * chip + w1 * j, 8)
        row2 = pl.multiple_of((n2 // 2) * core + u2 * chip + from2[j], 8)
        return (
            (0, (pl.ds(row1, w1), cols), (pl.ds(pl.multiple_of(base, 8), w1), cols)),
            (1, (pl.ds(row2, w2[j]), cols), (pl.ds(pl.multiple_of(base + w1, 8), w2[j]), cols)),
        )

    ins = (q1_ref, q2_ref)
    outs = (o1_ref, o2_ref)

    def stage(t):
        for j, d in RINGS:
            chip = here.owner(j, d, t + 1)
            for k, frm, to in pieces(here.core, chip, j, d):
                pltpu.make_async_copy(ins[k].at[frm], mine.at[to], stage_sem.at[t]).start()
            for k, frm, to in pieces(1 - here.core, chip, j, d):
                remote(ins[k].at[frm], part.at[to], pair_send.at[t], pair_recv.at[t], here.partner).start()

    def step(t, first, last):
        drain(mine.at[pl.ds(0, unit)], stage_sem.at[t])
        drain(part.at[pl.ds(0, unit)], pair_recv.at[t])
        for r, (j, d) in enumerate(RINGS):
            rows = pl.ds(pl.multiple_of(unit * here.owner(j, d, t + 1) + offs[j], 8), sizes[j])
            cols = pl.ds(256 * d, 256)
            block = mine.at[rows, cols]
            value = block[...] + part[rows, cols]
            if not first:
                slot = slots.at[t - 1, r, pl.ds(0, sizes[j])]
                drain(slot, ring_recv.at[t - 1, r])
                value = value + slot[...]
            block[...] = value
            if not last:
                remote(block, slots.at[t, r, pl.ds(0, sizes[j])], ring_send.at[t], ring_recv.at[t, r], here.target(j, d)).start()

    for t in range(AHEAD):
        stage(t)
    stage(AHEAD)
    step(0, True, False)

    def middle(t, carry):
        stage(t + AHEAD)
        step(t, False, False)
        return carry

    lax.fori_loop(1, CHIPS - AHEAD, middle, 0)
    lax.fori_loop(CHIPS - AHEAD, CHIPS - 1, lambda t, c: (step(t, False, False), c)[1], 0)
    step(CHIPS - 1, False, True)

    def gather_step(s, first, last):
        for r, (j, d) in enumerate(RINGS):
            cols = pl.ds(256 * d, 256)
            if not first:
                drain(mine.at[pl.ds(0, sizes[j]), cols], gat_recv.at[s - 1, r])
            for k, to, frm in pieces(here.core, here.owner(j, d, s), j, d):
                src = mine.at[frm] if first else outs[k].at[to]
                dst = outs[k].at[to]
                if first:
                    pltpu.make_async_copy(src, dst, out_sem.at[0]).start()
                if not last:
                    remote(src, dst, gat_send.at[s], gat_recv.at[s, r], here.target(j, d)).start()
                remote(src, dst, fwd_send.at[s], fwd_recv.at[s], here.partner).start()

    gather_step(0, True, False)
    lax.fori_loop(1, CHIPS - 1, lambda s, c: (gather_step(s, False, False), c)[1], 0)
    gather_step(CHIPS - 1, False, True)

    def settle(s, carry):
        drain(mine.at[pl.ds(0, unit)], fwd_recv.at[s])
        drain(mine.at[pl.ds(0, unit)], pair_send.at[s])
        drain(mine.at[pl.ds(0, unit)], fwd_send.at[s])
        return carry

    lax.fori_loop(0, CHIPS, settle, 0)

    def settle_rings(s, carry):
        drain(mine.at[pl.ds(0, unit)], ring_send.at[s])
        drain(mine.at[pl.ds(0, unit)], gat_send.at[s])
        return carry

    lax.fori_loop(0, CHIPS - 1, settle_rings, 0)
    drain(mine.at[pl.ds(0, unit)], out_sem.at[0])


def right_exchange(q1, q2):
    n1, rank = q1.shape
    n2 = q2.shape[0]
    unit = (n1 + n2) // 32
    dma = pltpu.SemaphoreType.DMA
    return pl.pallas_call(
        functools.partial(right_kernel, n1, n2),
        out_shape=(jax.ShapeDtypeStruct((n1, rank), jnp.float32), jax.ShapeDtypeStruct((n2, rank), jnp.float32)),
        in_specs=[pl.BlockSpec(memory_space=pl.ANY)] * 2,
        out_specs=(pl.BlockSpec(memory_space=pl.ANY),) * 2,
        scratch_shapes=[
            pltpu.VMEM((16 * unit, rank), jnp.float32),
            pltpu.VMEM((16 * unit, rank), jnp.float32),
            pltpu.VMEM((15, 6, 104, 256), jnp.float32),
            dma((16,)), dma((16,)), dma((16,)), dma((15,)), dma((15, 6)), dma((15,)), dma((15, 6)), dma((16,)), dma((16,)), dma((1,)),
        ],
        compiler_params=pltpu.CompilerParams(collective_id=1, has_side_effects=True, vmem_limit_bytes=60 * 2**20),
        name="right_exchange",
    )(q1, q2)


def gelu_tanh(values):
    return jax.nn.gelu(values, approximate=True)


def gelu_grad(pre_gelu, cot_gelu):
    pull_back = jax.vjp(gelu_tanh, pre_gelu)[1]
    return pull_back(cot_gelu)[0]


def mat_nn(left_op, right_op):
    return jnp.dot(left_op, right_op, preferred_element_type=jnp.float32)


def mat_nt(left_op, right_op):
    return lax.dot_general(left_op, right_op, (((1,), (1,)), ((), ())), preferred_element_type=jnp.float32)


def mat_tn(left_op, right_op):
    return lax.dot_general(left_op, right_op, (((0,), (0,)), ((), ())), preferred_element_type=jnp.float32)


def update_up_kernel(step_size, p_ref, q_ref, w_ref, *refs):
    o_ref, qo_ref, p_rows = refs[-3:]
    m = p_rows.shape[0]

    @pl.when(pl.program_id(0) == 0)
    def _():
        for i in range(0, m, 256):
            p_rows[pl.ds(i, 256)] = p_ref[:, pl.ds(i, 256)].T

    q = q_ref[...]
    qo_ref[0] = q
    q = q.astype(jnp.bfloat16)
    for i in range(0, m, 512):
        prod = mat_nt(p_rows[pl.ds(i, 512)], q)
        o_ref[0, pl.ds(i, 512)] = (w_ref[0, pl.ds(i, 512)].astype(jnp.float32) - step_size * prod).astype(jnp.bfloat16)


def update_down_kernel(step_size, p_ref, q_ref, w_ref, *refs):
    o_ref, qo_ref, q_cols = refs[-3:]
    n = q_cols.shape[1]

    @pl.when(pl.program_id(0) == 0)
    def _():
        qo_ref[0] = q_ref[...]
        for i in range(0, n, 256):
            q_cols[:, pl.ds(i, 256)] = q_ref[pl.ds(i, 256)].astype(jnp.bfloat16).T

    p = p_ref[...].T
    for i in range(0, n, 256):
        prod = mat_nn(p, q_cols[:, pl.ds(i, 256)])
        o_ref[0, :, pl.ds(i, 256)] = (w_ref[0, :, pl.ds(i, 256)].astype(jnp.float32) - step_size * prod).astype(jnp.bfloat16)


def update(up, p_hat, q_sum, weights, layer, prev, step_size, block):
    layers, m, n = weights.shape
    rank = p_hat.shape[0]
    if up:
        grid = n // block
        w_spec = pl.BlockSpec((1, m, block), lambda i: (layer, 0, i))
        specs = [pl.BlockSpec((rank, m), lambda i: (0, 0)), pl.BlockSpec((block, rank), lambda i: (i, 0)), w_spec]
        q_spec = pl.BlockSpec((1, block, rank), lambda i: (layer, i, 0))
        scratch = pltpu.VMEM((m, rank), jnp.bfloat16)
    else:
        grid = m // block
        w_spec = pl.BlockSpec((1, block, n), lambda i: (layer, i, 0))
        specs = [pl.BlockSpec((rank, block), lambda i: (0, i)), pl.BlockSpec((n, rank), lambda i: (0, 0)), w_spec]
        q_spec = pl.BlockSpec((1, n, rank), lambda i: (layer, 0, 0))
        scratch = pltpu.VMEM((rank, n), jnp.bfloat16)
    args = [p_hat, q_sum, weights]
    alias = {}
    if prev is not None:
        specs += [pl.BlockSpec(memory_space=pl.ANY)] * 2
        args += prev
        alias = {3: 0, 4: 1}
    return pl.pallas_call(
        functools.partial(update_up_kernel if up else update_down_kernel, step_size),
        grid=(grid,),
        out_shape=(jax.ShapeDtypeStruct(weights.shape, jnp.bfloat16), jax.ShapeDtypeStruct((layers, n, rank), jnp.float32)),
        in_specs=specs,
        out_specs=(w_spec, q_spec),
        scratch_shapes=[scratch],
        input_output_aliases=alias,
        compiler_params=pltpu.CompilerParams(dimension_semantics=("arbitrary",), vmem_limit_bytes=60 * 2**20),
        cost_estimate=pl.CostEstimate(flops=2 * m * n * rank, bytes_accessed=4 * m * n, transcendentals=0),
        name="update_up" if up else "update_down",
    )(*args)


def solution(mesh):
    def left(right_in, left_in, q_fac):
        sketch = mat_nn(right_in, q_fac).astype(jnp.bfloat16)
        return mat_tn(sketch, left_in)

    def right(right_in, left_in, p_hat):
        back_in = mat_nt(left_in, p_hat).astype(jnp.bfloat16)
        return mat_tn(right_in, back_in)

    def local_step(tok_rows, grad_rows, w_up, w_down, q_up, q_down):
        step_size = 0.4 / math.sqrt(q_up.shape[-1])
        z0 = mat_nn(tok_rows, w_up[0]).astype(jnp.bfloat16)
        a0 = gelu_tanh(z0.astype(jnp.float32)).astype(jnp.bfloat16)
        h1 = (tok_rows.astype(jnp.float32) + mat_nn(a0, w_down[0])).astype(jnp.bfloat16)
        z1 = mat_nn(h1, w_up[1]).astype(jnp.bfloat16)
        a1 = gelu_tanh(z1.astype(jnp.float32)).astype(jnp.bfloat16)
        e1 = gelu_grad(z1.astype(jnp.float32), mat_nt(grad_rows, w_down[1])).astype(jnp.bfloat16)
        pu1, pd1 = left_exchange(left(e1, h1, q_up[1]), left(grad_rows, a1, q_down[1]))
        g1 = (grad_rows.astype(jnp.float32) + mat_nt(e1, w_up[1])).astype(jnp.bfloat16)
        e0 = gelu_grad(z0.astype(jnp.float32), mat_nt(g1, w_down[0])).astype(jnp.bfloat16)
        pu0, pd0 = left_exchange(left(e0, tok_rows, q_up[0]), left(g1, a0, q_down[0]))
        qu1, qd1 = right_exchange(right(e1, h1, pu1), right(grad_rows, a1, pd1))
        qu0, qd0 = right_exchange(right(e0, tok_rows, pu0), right(g1, a0, pd0))
        up = update(True, pu1, qu1, w_up, 1, None, step_size, 384)
        down = update(False, pd1, qd1, w_down, 1, None, step_size, 768)
        up = update(True, pu0, qu0, w_up, 0, up, step_size, 384)
        down = update(False, pd0, qd0, w_down, 0, down, step_size, 768)
        return up[0], down[0], up[1], down[1]

    from jax.sharding import PartitionSpec as P
    row_spec = P(mesh.axis_names[0], None)
    return jax.shard_map(local_step, mesh=mesh, in_specs=(row_spec, row_spec, P(), P(), P(), P()), out_specs=(P(), P(), P(), P()), check_vma=False)
```

time: 1740 us -> 1050 us (0.60)
  waiting for transfers between devices: 1130 us -> 0 us
  Pallas kernels: 0 us -> 756 us
  matrix products: 445 us -> 288 us
  other arithmetic: 154 us -> 0 us
    psum x2 -> x0, waiting for transfers between devices: 1130 us -> none  [the longest x1 564 us: power_step(): p_sum = lax.psum(mat_tn(left_in, sketch), data_axis)]
    pallas_call x0 -> x8, Pallas kernels: none -> 756 us  [the longest x2 308 us: right_exchange(): pl.pallas_call(functools.partial(right_kernel, n1, n2), out_shape=(jax.Sh...]
    dot_general x7 -> x3, matrix products: 241 us -> 90.2 us  [mat_nt(): lax.dot_general(left_op, right_op, (((1,), (1,)), ((), ())), preferred_el...]
    another operation x4 -> x0, other arithmetic: 125 us -> none  [the longest x1 46.9 us: local_step(): jnp.stack(down_new)]
    reduce_sum x4 -> x0, other arithmetic: 18.6 us -> none  [col_normalise(): jnp.sum(p_sum * p_sum, axis=-2, keepdims=True)]
    dot_general x3 -> x5, matrix products: 88.5 us -> 92.9 us  [mat_nn(): return jnp.dot(left_op, right_op, preferred_element_type=jnp.float32)]
  transfers between devices with their start and end apart: 2 -> 0, of which waited for: 2 -> 0; matrix products, arithmetic and copies ran while one was open for 0% -> 0% of each run, Pallas kernels for 0% -> 0%
where the time goes in v1:
time: 1050 us; the launch traced here: 1040 us
  Pallas kernels  756 us (72%)
  matrix products  288 us (27%)
    pallas_call x2, Pallas kernels, right_exchange(): pl.pallas_call(functools.partial(right_kernel, n1, n2), out_shape=(jax.Sh...  308 us
    pallas_call x2, Pallas kernels, left_exchange(): pl.pallas_call(functools.partial(left_kernel, m1, m2), out_shape=(jax.Sha...  275 us
    pallas_call x4, Pallas kernels, update(): pl.pallas_call(functools.partial(update_up_kernel if up else update_down_...  173 us
    dot_general x8, matrix products, mat_tn(): lax.dot_general(left_op, right_op, (((0,), (0,)), ((), ())), preferred_el...  105 us
    dot_general x5, matrix products, mat_nn(): return jnp.dot(left_op, right_op, preferred_element_type=jnp.float32)  92.9 us
    dot_general x3, matrix products, mat_nt(): lax.dot_general(left_op, right_op, (((1,), (1,)), ((), ())), preferred_el...  90.2 us

profile of v1, /device:TPU:0, one launch (start us, length us, event | category | flops | bytes accessed | tf_op | source)
XLA Modules:
  0.0 1044.8 jit_solution(4672462561862347854)
XLA Ops:
  0.6 0.0 copy-start
  0.6 25.4 %fusion.38 = bf16[512,6912]{1,0:T(8,128)(2,1)} fusion(bf16[512,2560]{1,0:T(8,128)(2,1)} %param.6, bf16[2,2560,6912]{2,1,0:T(8,128)(2,1)} %w_ref.5), kind=kOutput, calls=%fused_computation.48 | convolution fusion | flops 18122932224 | bytes 45088768 | tf_op jit(solution)/shard_map/dot_general | solution.py:336
  26.1 0.0 copy-done
  26.1 34.6 %add_convert_fusion.1 = bf16[512,2560]{1,0:T(8,128)(2,1)} fusion(bf16[512,2560]{1,0:T(8,128)(2,1)S(1)} %copy-done, bf16[2,6912,2560]{2,1,0:T(8,128)(2,1)} %w_ref.7, bf16[512,6912]{1,0:T(8,128)(2,1)} %fusion.38), kind=kOutput, calls=%fused_computation.57 | convolution fusion | flops 18158714880 | bytes 47710208 | tf_op jit(solution)/shard_map/dot_general | solution.py:336
  60.7 0.0 copy-start.2
  60.7 25.6 %fusion.41 = bf16[512,6912]{1,0:T(8,128)(2,1)} fusion(bf16[512,2560]{1,0:T(8,128)(2,1)} %add_convert_fusion.1, bf16[2,2560,6912]{2,1,0:T(8,128)(2,1)} %w_ref.5), kind=kOutput, calls=%fused_computation.49 | convolution fusion | flops 18122932224 | bytes 45088768 | tf_op jit(solution)/shard_map/dot_general | solution.py:336
  86.3 0.0 copy-done.2
  86.3 32.0 %fusion.22 = bf16[512,6912]{1,0:T(8,128)(2,1)} fusion(bf16[512,6912]{1,0:T(8,128)(2,1)} %fusion.41, bf16[512,2560]{1,0:T(8,128)(2,1)S(1)} %copy-done.2, bf16[2,6912,2560]{2,1,0:T(8,128)(2,1)} %w_ref.7), kind=kOutput, calls=%fused_computation.32 | convolution fusion | flops 18193711104 | bytes 52166656 | tf_op jit(solution)/shard_map/dot_general | solution.py:340
  118.3 25.1 %add_convert_fusion = bf16[512,2560]{1,0:T(8,128)(2,1)} fusion(bf16[512,2560]{1,0:T(8,128)(2,1)S(1)} %copy-done.2, bf16[512,6912]{1,0:T(8,128)(2,1)} %fusion.22, bf16[2,2560,6912]{2,1,0:T(8,128)(2,1)} %w_ref.5), kind=kOutput, calls=%fused_computation.56 | convolution fusion | flops 18123325440 | bytes 47710208 | tf_op jit(solution)/shard_map/dot_general | solution.py:340
  143.4 0.0 copy-start.1
  143.4 33.1 %fusion.25 = bf16[512,6912]{1,0:T(8,128)(2,1)} fusion(bf16[512,6912]{1,0:T(8,128)(2,1)} %fusion.38, bf16[512,2560]{1,0:T(8,128)(2,1)} %add_convert_fusion, bf16[2,6912,2560]{2,1,0:T(8,128)(2,1)} %w_ref.7), kind=kOutput, calls=%fused_computation.35 | convolution fusion | flops 18193711104 | bytes 52166656 | tf_op jit(solution)/shard_map/dot_general | solution.py:340
  176.5 0.0 copy-done.1
  176.5 12.6 %fusion.82.p1_ref = f32[512,2560]{1,0:T(8,128)} fusion(bf16[512,2560]{1,0:T(8,128)(2,1)S(1)} %copy-done.1, bf16[512,6912]{1,0:T(8,128)(2,1)} %fusion.25, bf16[2,6912,512]{2,1,0:T(8,128)(2,1)} %param.10), kind=kOutput, calls=%fused_computation.76 | convolution fusion | flops 4966318080 | bytes 22020096 | tf_op jit(solution)/shard_map/dot_general | solution.py:344
  189.1 4.0 fusion.70
  193.2 11.5 %fusion.89.p2_ref = f32[512,6912]{1,0:T(8,128)} fusion(bf16[512,512]{1,0:T(8,128)(2,1)S(1)} %fusion.70, bf16[512,6912]{1,0:T(8,128)(2,1)} %fusion.38), kind=kOutput, calls=%fused_computation.78 | convolution fusion | flops 3659268096 | bytes 21757952 | tf_op jit(solution)/shard_map/dot_general | solution.py:344
  204.6 139.1 %left_exchange.2 = (bf16[512,2560]{1,0:T(8,128)(2,1)}, bf16[512,6912]{1,0:T(8,128)(2,1)}) custom-call(f32[512,2560]{1,0:T(8,128)} %fusion.82.p1_ref, f32[512,6912]{1,0:T(8,128)} %fusion.89.p2_ref), custom_call_target="tpu_custom_call" | custom-call | tf_op jit(solution)/shard_map/left_exchange/pallas_call | solution.py:190
  343.7 12.1 %fusion.77.q1_ref = f32[6912,512]{1,0:T(8,128)} fusion(bf16[512,6912]{1,0:T(8,128)(2,1)} %fusion.25, bf16[512,2560]{1,0:T(8,128)(2,1)} %get-tuple-element.20.p_ref, bf16[512,2560]{1,0:T(8,128)(2,1)S(1)} %copy-done.1), kind=kOutput, calls=%fused_computation.74 | convolution fusion | flops 4966318080 | bytes 26476544 | tf_op jit(solution)/shard_map/dot_general | solution.py:344
  355.8 14.5 %fusion.92.q2_ref = f32[2560,512]{1,0:T(8,128)} fusion(bf16[512,2560]{1,0:T(8,128)(2,1)} %add_convert_fusion, bf16[512,6912]{1,0:T(8,128)(2,1)} %get-tuple-element.21.p_ref, bf16[512,6912]{1,0:T(8,128)(2,1)} %fusion.38), kind=kOutput, calls=%fused_computation.79 | convolution fusion | flops 5001707520 | bytes 22020096 | tf_op jit(solution)/shard_map/dot_general | solution.py:344
  370.4 154.0 %right_exchange.2 = (f32[6912,512]{1,0:T(8,128)}, f32[2560,512]{1,0:T(8,128)}) custom-call(f32[6912,512]{1,0:T(8,128)} %fusion.77.q1_ref, f32[2560,512]{1,0:T(8,128)} %fusion.92.q2_ref), custom_call_target="tpu_custom_call" | custom-call | tf_op jit(solution)/shard_map/right_exchange/pallas_call | solution.py:310
  524.3 0.0 copy-start.3
  524.3 13.6 %fusion.79.p1_ref = f32[512,2560]{1,0:T(8,128)} fusion(bf16[512,2560]{1,0:T(8,128)(2,1)} %add_convert_fusion.1, bf16[512,6912]{1,0:T(8,128)(2,1)} %fusion.22, bf16[2,6912,512]{2,1,0:T(8,128)(2,1)} %param.10), kind=kOutput, calls=%fused_computation.75 | convolution fusion | flops 4966318080 | bytes 22020096 | tf_op jit(solution)/shard_map/dot_general | solution.py:344
  537.9 0.0 copy-done.3
  537.9 3.2 fusion.73
  541.1 11.5 %fusion.86.p2_ref = f32[512,6912]{1,0:T(8,128)} fusion(bf16[512,512]{1,0:T(8,128)(2,1)S(1)} %fusion.73, bf16[512,6912]{1,0:T(8,128)(2,1)} %fusion.41), kind=kOutput, calls=%fused_computation.77 | convolution fusion | flops 3659268096 | bytes 21757952 | tf_op jit(solution)/shard_map/dot_general | solution.py:344
  552.6 135.5 %left_exchange.3 = (bf16[512,2560]{1,0:T(8,128)(2,1)}, bf16[512,6912]{1,0:T(8,128)(2,1)}) custom-call(f32[512,2560]{1,0:T(8,128)} %fusion.79.p1_ref, f32[512,6912]{1,0:T(8,128)} %fusion.86.p2_ref), custom_call_target="tpu_custom_call" | custom-call | tf_op jit(solution)/shard_map/left_exchange/pallas_call | solution.py:190
  688.1 15.2 %fusion.76.q1_ref = f32[6912,512]{1,0:T(8,128)} fusion(bf16[512,6912]{1,0:T(8,128)(2,1)} %fusion.22, bf16[512,2560]{1,0:T(8,128)(2,1)} %add_convert_fusion.1, bf16[512,2560]{1,0:T(8,128)(2,1)} %get-tuple-element.23.p_ref), kind=kOutput, calls=%fused_computation.72 | convolution fusion | flops 4966318080 | bytes 26476544 | tf_op jit(solution)/shard_map/dot_general | solution.py:344
  703.2 13.9 %convolution_bitcast_fusion.q2_ref = f32[2560,512]{1,0:T(8,128)} fusion(bf16[512,2560]{1,0:T(8,128)(2,1)S(1)} %copy-done.3, bf16[512,6912]{1,0:T(8,128)(2,1)} %get-tuple-element.24.p_ref, bf16[512,6912]{1,0:T(8,128)(2,1)} %fusion.41), kind=kOutput, calls=%fused_computation.58 | convolution fusion | flops 5001707520 | bytes 22020096 | tf_op jit(solution)/shard_map/dot_general | solution.py:344
  717.1 154.0 %right_exchange.3 = (f32[6912,512]{1,0:T(8,128)}, f32[2560,512]{1,0:T(8,128)}) custom-call(f32[6912,512]{1,0:T(8,128)} %fusion.76.q1_ref, f32[2560,512]{1,0:T(8,128)} %convolution_bitcast_fusion.q2_ref), custom_call_target="tpu_custom_call" | custom-call | tf_op jit(solution)/shard_map/right_exchange/pallas_call | solution.py:310
  871.2 47.6 %update_up.2 = (bf16[2,2560,6912]{2,1,0:T(8,128)(2,1)}, f32[2,6912,512]{2,1,0:T(8,128)}) custom-call(bf16[512,2560]{1,0:T(8,128)(2,1)} %get-tuple-element.23.p_ref, f32[6912,512]{1,0:T(8,128)} %get-tuple-element.25.q_ref, bf16[2,2560,6912]{2,1,0:T(8,128)(2,1)} %w_ref.5), custom_call_target="tpu_custom_call" | custom-call | flops 18119393280 | bytes 70778880 | tf_op jit(solution)/shard_map/update_up/pallas_call | solution.py:401
  918.8 47.8 %update_up.3 = (bf16[2,2560,6912]{2,1,0:T(8,128)(2,1)}, f32[2,6912,512]{2,1,0:T(8,128)}) custom-call(bf16[512,2560]{1,0:T(8,128)(2,1)} %get-tuple-element.20.p_ref, f32[6912,512]{1,0:T(8,128)} %get-tuple-element.22.q_ref, bf16[2,2560,6912]{2,1,0:T(8,128)(2,1)} %w_ref.5, ...), custom_call_target="tpu_custom_call", output_to_operand_aliasing={{0}: (3, {}), {1}: (4, {})} | custom-call | flops 18119393280 | bytes 70778880 | tf_op jit(solution)/shard_map/update_up/pallas_call | solution.py:401
  966.6 38.9 %update_down.2 = (bf16[2,6912,2560]{2,1,0:T(8,128)(2,1)}, f32[2,2560,512]{2,1,0:T(8,128)}) custom-call(bf16[512,6912]{1,0:T(8,128)(2,1)} %get-tuple-element.24.p_ref, f32[2560,512]{1,0:T(8,128)} %get-tuple-element.30.q_ref, bf16[2,6912,2560]{2,1,0:T(8,128)(2,1)} %w_ref.7), custom_call_target="tpu_custom_call" | custom-call | flops 18119393280 | bytes 70778880 | tf_op jit(solution)/shard_map/update_down/pallas_call | solution.py:401
  1005.5 38.9 %update_down.3 = (bf16[2,6912,2560]{2,1,0:T(8,128)(2,1)}, f32[2,2560,512]{2,1,0:T(8,128)}) custom-call(bf16[512,6912]{1,0:T(8,128)(2,1)} %get-tuple-element.21.p_ref, f32[2560,512]{1,0:T(8,128)} %get-tuple-element.29.q_ref, bf16[2,6912,2560]{2,1,0:T(8,128)(2,1)} %w_ref.7, ...), custom_call_target="tpu_custom_call", output_to_operand_aliasing={{0}: (3, {}), {1}: (4, {})} | custom-call | flops 18119393280 | bytes 70778880 | tf_op jit(solution)/shard_map/update_down/pallas_call | solution.py:401
Async XLA Ops:
  0.6 25.4 %copy-start = (bf16[512,2560]{1,0:T(8,128)(2,1)S(1)}, bf16[512,2560]{1,0:T(8,128)(2,1)}, u32[]{:S(2)}) copy-start(bf16[512,2560]{1,0:T(8,128)(2,1)} %param.6) | copy-start | bytes 7864324
  60.7 25.6 %copy-start.2 = (bf16[512,2560]{1,0:T(8,128)(2,1)S(1)}, bf16[512,2560]{1,0:T(8,128)(2,1)}, u32[]{:S(2)}) copy-start(bf16[512,2560]{1,0:T(8,128)(2,1)} %param.7) | copy-start | bytes 7864324
  143.4 33.1 %copy-start.1 = (bf16[512,2560]{1,0:T(8,128)(2,1)S(1)}, bf16[512,2560]{1,0:T(8,128)(2,1)}, u32[]{:S(2)}) copy-start(bf16[512,2560]{1,0:T(8,128)(2,1)} %param.6) | copy-start | bytes 7864324
  524.3 13.6 %copy-start.3 = (bf16[512,2560]{1,0:T(8,128)(2,1)S(1)}, bf16[512,2560]{1,0:T(8,128)(2,1)}, u32[]{:S(2)}) copy-start(bf16[512,2560]{1,0:T(8,128)(2,1)} %param.7) | copy-start | bytes 7864324
